TPU v7x, 8 devices: a whole 2x2x1 slice. The times are simulated.
8 devices in a mesh: dp: 2 (over z, y), sp: 4 (over x, core).
Axes of the slice: x: 2, y: 2, z: 1, core: 2. Of those that a mesh axis runs over, the one named last changes fastest.
Arguments:
- tokens: bfloat16 [256, 2560], P('dp'), parts along dimension 0
- w_query: bfloat16 [2560, 2560], replicated
- w_key: bfloat16 [2560, 256], replicated
- w_value: bfloat16 [2560, 256], replicated
- w_out: bfloat16 [2560, 2560], P('sp')
- k_cache: bfloat16 [256, 2048, 256], P('dp', 'sp'), parts along dimension 0
- v_cache: bfloat16 [256, 2048, 256], P('dp', 'sp'), parts along dimension 0
- positions: int32 [256], P('dp'), parts along dimension 0
Outputs:
- output 1: bfloat16 [256, 2560], P('dp'), parts along dimension 0
- output 2: bfloat16 [256, 2048, 256], P('dp', 'sp'), parts along dimension 0
- output 3: bfloat16 [256, 2048, 256], P('dp', 'sp'), parts along dimension 0
There are 2 independent parts. A program takes and returns all parts, laid end to end along the dimension named above; an argument that names none is the same for every part.
All inputs are finite; a program needn't handle non-finite values.
Results may differ from a plain program's by a relative error of at most 0.00402993.
Values are sent between devices in bfloat16 or wider.
A program may use at most 1 GiB of HBM per device.

v0:
```python
import jax
import jax.numpy as jnp
from jax import lax
from jax.sharding import PartitionSpec as P


def solution(mesh):
    def local_step(tokens, w_query, w_key, w_value, w_out, k_cache, v_cache, positions):
        n_rows, seq_local, head_dim = k_cache.shape
        q_width = w_query.shape[1]
        n_heads = q_width // head_dim
        rows_local = w_out.shape[0]
        shard_idx = lax.axis_index('sp')
        queries = jnp.dot(tokens, w_query, preferred_element_type=jnp.float32).astype(jnp.bfloat16).reshape(n_rows, n_heads, head_dim)
        key_new = jnp.dot(tokens, w_key, preferred_element_type=jnp.float32).astype(jnp.bfloat16)
        value_new = jnp.dot(tokens, w_value, preferred_element_type=jnp.float32).astype(jnp.bfloat16)
        local_pos = positions - shard_idx * seq_local
        slot_ids = jnp.arange(seq_local)
        hit_mask = (slot_ids[None, :] == local_pos[:, None])[:, :, None]
        k_upd = jnp.where(hit_mask, key_new[:, None, :], k_cache)
        v_upd = jnp.where(hit_mask, value_new[:, None, :], v_cache)
        scores = jnp.einsum('bhd,btd->bht', queries, k_upd, preferred_element_type=jnp.float32) * head_dim ** -0.5
        valid_mask = (slot_ids[None, :] <= local_pos[:, None])[:, None, :]
        scores = jnp.where(valid_mask, scores, -jnp.inf)
        row_peak = jnp.maximum(jnp.max(scores, axis=2), -1e30)
        weights = jnp.exp(scores - row_peak[:, :, None])
        weight_sum = jnp.sum(weights, axis=2)
        value_sum = jnp.einsum('bht,btd->bhd', weights.astype(jnp.bfloat16), v_upd, preferred_element_type=jnp.float32)
        peak_all = lax.pmax(row_peak, 'sp')
        rescale = jnp.exp(row_peak - peak_all)
        weight_all = lax.psum(weight_sum * rescale, 'sp')
        value_all = lax.psum(value_sum * rescale[:, :, None], 'sp')
        attn_heads = (value_all / weight_all[:, :, None]).astype(jnp.bfloat16).reshape(n_rows, q_width)
        attn_local = lax.dynamic_slice_in_dim(attn_heads, shard_idx * rows_local, rows_local, axis=1)
        partial = jnp.dot(attn_local, w_out, preferred_element_type=jnp.float32)
        attn_out = lax.psum(partial, 'sp').astype(jnp.bfloat16)
        return attn_out, k_upd, v_upd

    cache_spec = P('dp', 'sp', None)
    return jax.shard_map(local_step, mesh=mesh, in_specs=(P('dp', None), P(), P(), P(), P('sp', None), cache_spec, cache_spec, P('dp')), out_specs=(P('dp', None), cache_spec, cache_spec), check_vma=False)
```

profile of v0, /device:TPU:0, one launch (start us, length us, event | category | flops | bytes accessed | tf_op | source)
XLA Modules:
  0.0 211.9 jit_solution(6417295276125414283)
XLA Ops:
  7.2 0.0 copy-start
  7.2 0.0 all-reduce.3.cloned.1.call-start
  7.2 2.0 convolution_convert_fusion.2
  9.2 1.9 convolution_convert_fusion.1
  11.1 0.7 broadcast_subtract_fusion
  11.8 0.1 iota_compare_fusion.1
  11.9 7.7 %convolution_convert_fusion = bf16[128,2560]{1,0:T(8,128)(2,1)} fusion(bf16[128,2560]{1,0:T(8,128)(2,1)} %param.8, bf16[2560,2560]{1,0:T(8,128)(2,1)} %param.9), kind=kOutput, calls=%fused_computation.5 | convolution fusion | flops 1678049280 | bytes 14417920 | tf_op jit(solution)/shard_map/dot_general | solution.py:14
  19.6 2.2 %copy.11 = bf16[128,2560]{0,1:T(8,128)(2,1)} copy(bf16[128,2560]{1,0:T(8,128)(2,1)} %convolution_convert_fusion) | data formatting | bytes 1310720 | tf_op jit(solution)/shard_map/convert_element_type | solution.py:14
  21.8 2.6 %copy.12 = bf16[128,10,256]{2,1,0:T(8,128)(2,1)} copy(bf16[128,10,256]{0,2,1:T(8,128)(2,1)} %bitcast.12) | data formatting | bytes 1310720 | tf_op jit(solution)/shard_map/reshape | solution.py:14
  24.3 44.5 %broadcast_select_fusion.1 = (bf16[128,512,256]{2,1,0:T(8,128)(2,1)}, bf16[128,512,256]{2,1,0:T(8,128)(2,1)}) fusion(bf16[128,512,256]{2,1,0:T(8,128)(2,1)} %param.13, pred[128,512]{1,0:T(8,128)(4,1)S(1)} %get-tuple-element.8, bf16[128,256]{1,0:T(8,128)(2,1)S(1)} %convolution_convert_fusion.2, bf16[128,512,256]{2,1,0:T(8,128)(2,1)} %param.14, ...), kind=kLoop, calls=%fused_computation.1 | loop fusion | flops 33554432 | bytes 134414336 | tf_op jit(solution)/shard_map/jit(_where)/select_n | solution.py:20
  68.9 0.0 copy-done.1
  68.9 16.8 %fusion = (f32[128,10]{1,0:T(8,128)S(1)}, f32[128,10,512]{2,1,0:T(8,128)}) fusion(pred[128,512]{1,0:T(8,128)(4,1)S(1)} %get-tuple-element.7, bf16[128,10,256]{2,1,0:T(8,128)(2,1)S(1)} %copy-done.1, bf16[128,512,256]{2,1,0:T(8,128)(2,1)} %get-tuple-element.5), kind=kOutput, calls=%fused_computation.4 | convolution fusion | flops 337509120 | bytes 36901888 | tf_op jit(solution)/shard_map/bhd,btd->bht/dot_general | solution.py:22
  85.6 14.4 %pmax.7 = f32[128,10]{1,0:T(8,128)} all-reduce(f32[128,10]{1,0:T(8,128)S(1)} %broadcast_maximum_fusion), channel_id=1, replica_groups=mesh['dp'=2,'sp'=4] {'sp'}, use_global_device_ids=true, to_apply=%region_1.2 | all-reduce | flops 1280 | bytes 10240 | tf_op jit(solution)/shard_map/pmax | solution.py:29
  100.0 3.0 %fusion.1 = f32[128,10]{1,0:T(8,128)S(1)} fusion(f32[128,10,512]{2,1,0:T(8,128)} %get-tuple-element.10, f32[128,10]{1,0:T(8,128)S(1)} %broadcast_maximum_fusion, pred[128,512]{1,0:T(8,128)(4,1)S(1)} %get-tuple-element.7), kind=kLoop, calls=%fused_computation.6 | loop fusion | flops 2620160 | bytes 2697216 | tf_op jit(solution)/shard_map/reduce_sum | solution.py:27
  103.1 0.7 fusion.17
  103.7 18.2 %fusion.9 = f32[128,10,256]{2,1,0:T(8,128)} fusion(bf16[128,512,256]{2,1,0:T(8,128)(2,1)} %get-tuple-element.6, f32[128,10,512]{2,1,0:T(8,128)} %get-tuple-element.10, f32[128,10]{1,0:T(8,128)S(1)} %broadcast_maximum_fusion, pred[128,512]{1,0:T(8,128)(4,1)S(1)} %get-tuple-element.7, f32[128,10]{1,0:T(8,128)S(1)} %get-tuple-element.4), kind=kOutput, calls=%fused_computation.14 | convolution fusion | flops 338493440 | bytes 37562368 | tf_op jit(solution)/shard_map/bht,btd->bhd/dot_general | solution.py:28
  122.0 0.0 all-reduce.3.cloned.1.call-update
  122.0 12.1 %psum.22 = f32[128,10]{1,0:T(8,128)S(1)} all-reduce(f32[128,10]{1,0:T(8,128)S(1)} %copy-done.2), channel_id=1, replica_groups=mesh['dp'=2,'sp'=4] {'sp'}, use_global_device_ids=true, to_apply=%region_4.5 | all-reduce | flops 1280 | bytes 10240 | tf_op jit(solution)/shard_map/psum | solution.py:31
  134.1 34.5 %all-reduce.3.cloned.1.call-done = f32[128,10,256]{2,1,0:T(8,128)} async-done(((f32[128,10,256]{2,1,0:T(8,128)}), f32[128,10,256]{2,1,0:T(8,128)}) %all-reduce.3.cloned.1.call-update) | async-done | bytes 1310736 | tf_op jit(solution)/shard_map/psum | solution.py:32
  168.6 2.9 %divide_convert_fusion = bf16[128,10,256]{2,1,0:T(8,128)(2,1)} fusion(f32[128,10,256]{2,1,0:T(8,128)} %all-reduce.3.cloned.1.call-done, f32[128,10]{1,0:T(8,128)S(1)} %psum.22), kind=kLoop, calls=%fused_computation.9 | loop fusion | flops 655360 | bytes 1971200 | tf_op jit(solution)/shard_map/convert_element_type | solution.py:33
  171.5 2.4 %copy.13 = bf16[128,10,256]{0,2,1:T(8,128)(2,1)} copy(bf16[128,10,256]{2,1,0:T(8,128)(2,1)} %divide_convert_fusion) | data formatting | bytes 1310720 | tf_op jit(solution)/shard_map/convert_element_type | solution.py:33
  173.9 0.0 copy-done
  173.9 2.7 %fusion.12 = f32[128,2560]{1,0:T(8,128)} fusion(bf16[640,2560]{1,0:T(8,128)(2,1)S(1)} %copy-done, bf16[128,2560]{0,1:T(8,128)(2,1)} %bitcast.13, s32[]{:T(128)S(6)} %select_n.17), kind=kOutput, calls=%fused_computation.19 | convolution fusion | flops 419430400 | bytes 4751364 | tf_op jit(solution)/shard_map/dot_general | solution.py:35
  176.6 28.4 %all-reduce.4 = bf16[128,2560]{1,0:T(8,128)(2,1)} all-reduce(f32[128,2560]{1,0:T(8,128)} %fusion.12), channel_id=1, replica_groups=mesh['dp'=2,'sp'=4] {'sp'}, use_global_device_ids=true, to_apply=%region_5.6 | all-reduce | flops 327680 | bytes 1966080 | tf_op jit(solution)/shard_map/psum | solution.py:36
  (6 shorter events, 0.0 us)
Async XLA Ops:
  7.2 166.8 %copy-start = (bf16[640,2560]{1,0:T(8,128)(2,1)S(1)}, bf16[640,2560]{1,0:T(8,128)(2,1)}, u32[]{:S(2)}) copy-start(bf16[640,2560]{1,0:T(8,128)(2,1)} %param.12) | copy-start | bytes 9830404
  7.2 161.4 %all-reduce.3.cloned.1.call-start = ((), (), s32[]{:S(2)}) async-start(), calls=%async_computation | async-start | bytes 4194304 | tf_op jit(solution)/shard_map/psum | solution.py:32
  24.3 44.5 %copy-start.1 = (bf16[128,10,256]{2,1,0:T(8,128)(2,1)S(1)}, bf16[128,10,256]{2,1,0:T(8,128)(2,1)}, u32[]{:S(2)}) copy-start(bf16[128,10,256]{2,1,0:T(8,128)(2,1)} %copy.12) | copy-start | bytes 1966084
  100.0 3.0 %copy-start.3 = (f32[128,10]{1,0:T(8,128)S(1)}, f32[128,10]{1,0:T(8,128)}, u32[]{:S(2)}) copy-start(f32[128,10]{1,0:T(8,128)} %pmax.7) | copy-start | bytes 15364
  103.7 18.3 %copy-start.2 = (f32[128,10]{1,0:T(8,128)S(1)}, f32[128,10]{1,0:T(8,128)}, u32[]{:S(2)}) copy-start(f32[128,10]{1,0:T(8,128)} %get-tuple-element.3) | copy-start | bytes 15364
Sparse Core Ops, SparseCore 0:
  122.1 46.4 all-reduce.2
where the time goes:
time: 212 us
  blocking collectives  54.9 us (26%)
  other arithmetic  51.9 us (24%)
  matrix products  49.2 us (23%)
  waiting for transfers between devices  34.6 us (16%)
  between operations  14.1 us (7%)
  local copies, waits for them, and re-layouts  7.16 us (3%)
    select_n x1, other arithmetic, local_step(): k_upd = jnp.where(hit_mask, key_new[:, None, :], k_cache)  44.5 us
    psum x1, waiting for transfers between devices, local_step(): value_all = lax.psum(value_sum * rescale[:, :, None], 'sp')  34.5 us
    psum x1, blocking collectives, local_step(): attn_out = lax.psum(partial, 'sp').astype(jnp.bfloat16)  28.4 us
    dot_general x1, matrix products, local_step(): jnp.einsum('bht,btd->bhd', weights.astype(jnp.bfloat16), v_upd, preferred...  18.2 us
    dot_general x1, matrix products, local_step(): jnp.einsum('bhd,btd->bht', queries, k_upd, preferred_element_type=jnp.flo...  16.8 us
    pmax x1, blocking collectives, local_step(): peak_all = lax.pmax(row_peak, 'sp')  14.4 us
    psum x1, blocking collectives, local_step(): weight_all = lax.psum(weight_sum * rescale, 'sp')  12.1 us
    dot_general x1, matrix products, local_step(): jnp.dot(tokens, w_query, preferred_element_type=jnp.float32)  7.66 us
  transfers between devices with their start and end apart: 1, of which 1 were waited for; matrix products, arithmetic and copies ran while one was open for 0% of the time, Pallas kernels for 0%

commit v1 on v0

v1 whole, which is shorter than its diff:
```python
import functools
import jax
import jax.numpy as jnp
from jax import lax
from jax.sharding import PartitionSpec as P
from jax.experimental import pallas as pl
from jax.experimental.pallas import tpu as pltpu

MESH = pl.DeviceIdType.MESH
F32 = jnp.float32
BF16 = jnp.bfloat16
HEAD_PAD = 16
BLOCK_ROWS = 8
SLOTS = 8
WRITE_LAG = 2
COL_CHUNK = 512


def attention_kernel(n_heads, pos_ref, tok_hbm, wq_hbm, wk_hbm, wv_hbm, wo_hbm, k_hbm, v_hbm,
                     ko_hbm, vo_hbm, o_ref, ml_ref, wo_ref,
                     tok, wq, wk, wv, q_scr, kn_scr, vn_scr, s_scr, w_scr, kbuf, vbuf,
                     wo_sem, w_sems, wq_sems, kin_sems, vin_sems, kout_sems, vout_sems):
    n_rows, seq_local, head_dim = k_hbm.shape
    n_blocks = n_rows // BLOCK_ROWS
    n_slots = kbuf.shape[0]
    base = lax.axis_index('sp') * seq_local
    scale = head_dim ** -0.5

    def reads(blk, slot):
        rows = pl.ds(blk * BLOCK_ROWS, BLOCK_ROWS)
        return (pltpu.make_async_copy(k_hbm.at[rows], kbuf.at[slot], kin_sems.at[slot]),
                pltpu.make_async_copy(v_hbm.at[rows], vbuf.at[slot], vin_sems.at[slot]))

    def writes(blk, slot):
        rows = pl.ds(blk * BLOCK_ROWS, BLOCK_ROWS)
        return (pltpu.make_async_copy(kbuf.at[slot], ko_hbm.at[rows], kout_sems.at[slot]),
                pltpu.make_async_copy(vbuf.at[slot], vo_hbm.at[rows], vout_sems.at[slot]))

    small = [pltpu.make_async_copy(s, d, w_sems.at[i])
             for i, (s, d) in enumerate(((tok_hbm, tok), (wk_hbm, wk), (wv_hbm, wv)))]
    n_chunks = wq.shape[1] // COL_CHUNK
    big = [pltpu.make_async_copy(wq_hbm.at[:, pl.ds(i * COL_CHUNK, COL_CHUNK)],
                                 wq.at[:, pl.ds(i * COL_CHUNK, COL_CHUNK)], wq_sems.at[i])
           for i in range(n_chunks)]
    for c in small + big:
        c.start()
    for s in range(n_slots):
        for c in reads(s, s):
            c.start()
    load_wo = pltpu.make_async_copy(wo_hbm, wo_ref, wo_sem)
    load_wo.start()

    half = head_dim // 2
    for j in range(2):
        q_scr[j, pl.ds(n_heads * n_rows, (HEAD_PAD - n_heads) * n_rows), :] = jnp.zeros(
            ((HEAD_PAD - n_heads) * n_rows, half), F32)
    for c in small:
        c.wait()

    def project(w):
        return jnp.dot(tok[...], w, preferred_element_type=F32).astype(BF16).astype(F32)

    kn_scr[...] = project(wk[...])
    vn_scr[...] = project(wv[...])
    per_chunk = COL_CHUNK // head_dim
    for i in range(n_chunks):
        big[i].wait()
        for h in range(i * per_chunk, (i + 1) * per_chunk):
            q_head = project(wq[:, pl.ds(h * head_dim, head_dim)])
            for j in range(2):
                q_scr[j, pl.ds(h * n_rows, n_rows), :] = q_head[:, j * half:(j + 1) * half]

    lane_t = lax.broadcasted_iota(jnp.int32, (HEAD_PAD, seq_local), 1)
    lane_b = lax.broadcasted_iota(jnp.int32, (HEAD_PAD, n_rows), 1)
    sub16 = lax.broadcasted_iota(jnp.int32, (16, head_dim), 0)

    def block(blk, carry):
        m_acc, l_acc = carry
        slot = lax.rem(blk, n_slots)
        for c in reads(blk, slot):
            c.wait()
        for i in range(BLOCK_ROWS):
            b = blk * BLOCK_ROWS + i
            local = pos_ref[b] - base
            start = pl.multiple_of(jnp.clip(local // 16, 0, seq_local // 16 - 1) * 16, 16)
            for buf, new in ((kbuf, kn_scr), (vbuf, vn_scr)):
                tile = buf[slot, i, pl.ds(start, 16), :].astype(F32)
                row = new[pl.ds(b, 1), :]
                buf[slot, i, pl.ds(start, 16), :] = jnp.where(
                    sub16 == local - start, jnp.broadcast_to(row, (16, head_dim)), tile).astype(BF16)
        for i in range(BLOCK_ROWS):
            b = blk * BLOCK_ROWS + i
            q = jnp.concatenate([q_scr[j, pl.ds(b, HEAD_PAD, stride=n_rows), :] for j in range(2)],
                                axis=1).astype(BF16)
            s_scr[i] = lax.dot_general(q, kbuf[slot, i], (((1,), (1,)), ((), ())),
                                       preferred_element_type=F32)
        for i in range(BLOCK_ROWS):
            b = blk * BLOCK_ROWS + i
            local = pos_ref[b] - base
            s = jnp.where(lane_t <= local, s_scr[i] * scale, -jnp.inf)
            m = jnp.maximum(jnp.max(s, axis=1, keepdims=True), -1e30)
            w = jnp.exp(s - m)
            l = jnp.sum(w, axis=1, keepdims=True)
            w_scr[i] = w.astype(BF16)
            m_acc = jnp.where(lane_b == b, m, m_acc)
            l_acc = jnp.where(lane_b == b, l, l_acc)
        for i in range(BLOCK_ROWS):
            b = blk * BLOCK_ROWS + i
            o = jnp.dot(w_scr[i], vbuf[slot, i], preferred_element_type=F32)
            for j in range(2):
                o_ref[pl.ds(j * n_rows + b, HEAD_PAD, stride=2 * n_rows), :] = o[:, j * half:(j + 1) * half]
        for c in writes(blk, slot):
            c.start()

        @pl.when(jnp.logical_and(blk >= WRITE_LAG, blk - WRITE_LAG + n_slots < n_blocks))
        def _():
            old = blk - WRITE_LAG
            old_slot = lax.rem(old, n_slots)
            for c in writes(old, old_slot):
                c.wait()
            for c in reads(old + n_slots, old_slot):
                c.start()

        return m_acc, l_acc

    zero = jnp.zeros((HEAD_PAD, n_rows), F32)
    load_wo.wait()
    m_acc, l_acc = lax.fori_loop(0, n_blocks, block, (zero, zero))
    ml_ref[pl.ds(0, HEAD_PAD), :] = m_acc
    ml_ref[pl.ds(HEAD_PAD, HEAD_PAD), :] = l_acc
    for blk in range(n_blocks - n_slots, n_blocks):
        for c in writes(blk, blk % n_slots):
            c.wait()


def attention(pos, tok, wq, wk, wv, wo, k, v):
    n_rows, seq_local, head_dim = k.shape
    d_model, q_width = wq.shape
    n_heads = q_width // head_dim
    any_spec = pl.BlockSpec(memory_space=pl.ANY)
    vmem_spec = pl.BlockSpec(memory_space=pltpu.VMEM)
    dma = pltpu.SemaphoreType.DMA
    n_slots = min(SLOTS, n_rows // BLOCK_ROWS)
    return pl.pallas_call(
        functools.partial(attention_kernel, n_heads),
        out_shape=(jax.ShapeDtypeStruct(k.shape, k.dtype), jax.ShapeDtypeStruct(v.shape, v.dtype),
                   pltpu.VMEM((2 * HEAD_PAD * n_rows, head_dim // 2), F32),
                   pltpu.VMEM((2 * HEAD_PAD, n_rows), F32), pltpu.VMEM(wo.shape, BF16)),
        in_specs=[pl.BlockSpec(memory_space=pltpu.SMEM)] + [any_spec] * 7,
        out_specs=(any_spec, any_spec, vmem_spec, vmem_spec, vmem_spec),
        scratch_shapes=[
            pltpu.VMEM(tok.shape, BF16), pltpu.VMEM(wq.shape, BF16),
            pltpu.VMEM(wk.shape, BF16), pltpu.VMEM(wv.shape, BF16),
            pltpu.VMEM((2, HEAD_PAD * n_rows, head_dim // 2), F32),
            pltpu.VMEM((n_rows, head_dim), F32), pltpu.VMEM((n_rows, head_dim), F32),
            pltpu.VMEM((BLOCK_ROWS, HEAD_PAD, seq_local), F32),
            pltpu.VMEM((BLOCK_ROWS, HEAD_PAD, seq_local), BF16),
            pltpu.VMEM((n_slots, BLOCK_ROWS, seq_local, head_dim), BF16),
            pltpu.VMEM((n_slots, BLOCK_ROWS, seq_local, head_dim), BF16),
            dma, dma((3,)), dma((q_width // COL_CHUNK,)),
            dma((n_slots,)), dma((n_slots,)), dma((n_slots,)), dma((n_slots,))],
        compiler_params=pltpu.CompilerParams(vmem_limit_bytes=54 * 1024 * 1024),
        cost_estimate=pl.CostEstimate(flops=10**10, bytes_accessed=150 * 10**6, transcendentals=0),
        name='attention',
    )(pos, tok, wq, wk, wv, wo, k, v)


def combine_kernel(o_ref, ml_ref, wo, y_ref,
                   po, pml, oc, mlc, om, xo, xml, fbuf, ob, yq, yp, ym, yx, yxr, yb, yg,
                   send, recv):
    n_rows = y_ref.shape[0]
    rows_local, d_model = wo.shape
    units = rows_local // 128
    span = units * n_rows
    quarter = d_model // 4
    me = lax.axis_index('sp')
    core = lax.rem(me, 2)
    chip = me // 2
    partner = chip * 2 + 1 - core
    cross = (1 - chip) * 2 + core

    barrier = pltpu.get_barrier_semaphore()
    for peer in (partner, cross):
        pl.semaphore_signal(barrier, inc=1, device_id={'sp': peer}, device_id_type=MESH)
    pl.semaphore_wait(barrier, 2)

    def remote(i, src, dst, peer):
        return pltpu.make_async_remote_copy(src_ref=src, dst_ref=dst, send_sem=send.at[i], recv_sem=recv.at[i],
                                            device_id={'sp': peer}, device_id_type=MESH)

    def part(dest):
        return o_ref.at[pl.ds(pl.multiple_of(dest * span, span), span)]

    far, near = (1 - chip) * 2, chip * 2
    p_ml = remote(0, ml_ref, pml, partner)
    p_far = remote(1, part(far + 1 - core), po.at[0], partner)
    p_near = remote(2, part(near + 1 - core), po.at[1], partner)
    for c in (p_ml, p_far, p_near):
        c.start()

    def merge(a, b):
        peak = jnp.maximum(a[:HEAD_PAD], b[:HEAD_PAD])
        fa = jnp.exp(a[:HEAD_PAD] - peak)
        fb = jnp.exp(b[:HEAD_PAD] - peak)
        return fa, fb, peak, a[HEAD_PAD:] * fa + b[HEAD_PAD:] * fb

    def columns(k, dest):
        picks = [fbuf[k, pl.ds((dest * units + u) // 2, 1), :] for u in range(units)]
        picks += [picks[-1]] * (8 - units)
        return jnp.concatenate(picks, axis=0).T

    p_ml.wait_recv()
    fa, fb, peak, total = merge(ml_ref[...], pml[...])
    fbuf[0] = fa
    fbuf[1] = fb
    mlc[pl.ds(0, HEAD_PAD), :] = peak
    mlc[pl.ds(HEAD_PAD, HEAD_PAD), :] = total
    x_ml = remote(3, mlc, xml, cross)
    x_ml.start()

    def chip_part(dest, slot, dst):
        ca, cb = columns(0, dest), columns(1, dest)
        for u in range(units):
            mine = o_ref[pl.ds(pl.multiple_of(dest * span + u * n_rows, n_rows), n_rows), :]
            theirs = po[slot, pl.ds(u * n_rows, n_rows), :]
            dst[pl.ds(u * n_rows, n_rows), :] = mine * ca[:, u:u + 1] + theirs * cb[:, u:u + 1]

    p_far.wait_recv()
    chip_part(far + core, 0, oc)
    x_o = remote(4, oc, xo, cross)
    x_o.start()
    p_near.wait_recv()
    chip_part(me, 1, om)

    x_ml.wait_recv()
    fa, fb, peak, total = merge(mlc[...], xml[...])
    fbuf[2] = fa
    fbuf[3] = fb
    fbuf[4] = total
    ca, cb, cl = columns(2, me), columns(3, me), columns(4, me)
    x_o.wait_recv()
    for u in range(units):
        rows = pl.ds(u * n_rows, n_rows)
        value = om[rows, :] * ca[:, u:u + 1] + xo[rows, :] * cb[:, u:u + 1]
        ob[:, u * 128:(u + 1) * 128] = (value / cl[:, u:u + 1]).astype(BF16)

    def product(c, x):
        cols = pl.ds(pl.multiple_of((c * 2 + x) * quarter, quarter), quarter)
        return jnp.dot(ob[...], wo[:, cols], preferred_element_type=F32)

    yq[0] = product(1 - core, 1 - chip)
    p_y0 = remote(5, yq.at[0], yp.at[0], partner)
    p_y0.start()
    yq[1] = product(1 - core, chip)
    p_y1 = remote(6, yq.at[1], yp.at[1], partner)
    p_y1.start()
    ym[...] = product(core, 1 - chip)
    p_y0.wait_recv()
    yx[...] = ym[...] + yp[0]
    x_y = remote(7, yx, yxr, cross)
    x_y.start()
    ym[...] = product(core, chip)
    p_y1.wait_recv()
    ym[...] = ym[...] + yp[1]
    x_y.wait_recv()
    yb[...] = (ym[...] + yxr[...]).astype(BF16)
    x_b = remote(8, yb, yg.at[0], cross)
    p_b = remote(9, yb, yg.at[1], partner)
    x_b.start()
    p_b.start()
    x_b.wait_recv()
    p_f = remote(10, yg.at[0], yg.at[2], partner)
    p_f.start()

    def place(c, x, value):
        y_ref[:, pl.ds(pl.multiple_of((c * 2 + x) * quarter, quarter), quarter)] = value

    place(core, chip, yb[...])
    place(core, 1 - chip, yg[0])
    p_b.wait_recv()
    place(1 - core, chip, yg[1])
    p_f.wait_recv()
    place(1 - core, 1 - chip, yg[2])
    for c in (p_ml, p_far, p_near, x_ml, x_o, p_y0, p_y1, x_y, x_b, p_b, p_f):
        c.wait_send()


def combine(o, ml, w_out, n_rows):
    rows_local, d_model = w_out.shape
    units = rows_local // 128
    span = units * n_rows
    quarter = d_model // 4
    vmem = pl.BlockSpec(memory_space=pltpu.VMEM)
    part = pltpu.VMEM((span, 128), F32)
    tail = pltpu.VMEM((n_rows, quarter), F32)
    return pl.pallas_call(
        combine_kernel,
        out_shape=jax.ShapeDtypeStruct((n_rows, d_model), BF16),
        in_specs=[vmem, vmem, vmem],
        out_specs=vmem,
        scratch_shapes=[
            pltpu.VMEM((2, span, 128), F32), pltpu.VMEM(ml.shape, F32),
            part, pltpu.VMEM(ml.shape, F32), part, part, pltpu.VMEM(ml.shape, F32),
            pltpu.VMEM((5, HEAD_PAD, n_rows), F32), pltpu.VMEM((n_rows, rows_local), BF16),
            pltpu.VMEM((2, n_rows, quarter), F32), pltpu.VMEM((2, n_rows, quarter), F32),
            tail, tail, tail, pltpu.VMEM((n_rows, quarter), BF16), pltpu.VMEM((3, n_rows, quarter), BF16),
            pltpu.SemaphoreType.DMA((11,)), pltpu.SemaphoreType.DMA((11,))],
        compiler_params=pltpu.CompilerParams(collective_id=0, has_side_effects=True,
                                             vmem_limit_bytes=40 * 1024 * 1024),
        name='combine',
    )(o, ml, w_out)


def solution(mesh):
    def local_step(tokens, w_query, w_key, w_value, w_out, k_cache, v_cache, positions):
        k_upd, v_upd, o, ml, wo = attention(positions, tokens, w_query, w_key, w_value, w_out, k_cache, v_cache)
        attn_out = combine(o, ml, wo, k_cache.shape[0])
        return attn_out, k_upd, v_upd

    cache_spec = P('dp', 'sp', None)
    return jax.shard_map(local_step, mesh=mesh, in_specs=(P('dp', None), P(), P(), P(), P('sp', None), cache_spec, cache_spec, P('dp')), out_specs=(P('dp', None), cache_spec, cache_spec), check_vma=False)
```

time: 212 us -> 85.2 us (0.40)
  Pallas kernels: 0 us -> 83.6 us
  blocking collectives: 54.9 us -> 0 us
  other arithmetic: 51.9 us -> 0 us
  matrix products: 49.2 us -> 0 us
  waiting for transfers between devices: 34.6 us -> 0 us
  between operations: 14.1 us -> 0.65 us
  local copies, waits for them, and re-layouts: 7.16 us -> 0.84 us
    pallas_call x0 -> x2, Pallas kernels: none -> 83.6 us  [the longest x1 52.9 us: attention(): pl.pallas_call(functools.partial(attention_kernel, n_heads), out_shape=(j...]
    dot_general x6 -> x0, matrix products: 49.2 us -> none  [the longest x1 18.2 us: local_step(): jnp.einsum('bht,btd->bhd', weights.astype(jnp.bfloat16), v_upd, preferred...]
    select_n x1 -> x0, other arithmetic: 44.5 us -> none  [local_step(): k_upd = jnp.where(hit_mask, key_new[:, None, :], k_cache)]
    psum x2 -> x0, blocking collectives: 40.5 us -> none  [the longest x1 28.4 us: local_step(): attn_out = lax.psum(partial, 'sp').astype(jnp.bfloat16)]
    psum x1 -> x0, waiting for transfers between devices: 34.5 us -> none  [local_step(): value_all = lax.psum(value_sum * rescale[:, :, None], 'sp')]
    pmax x1 -> x0, blocking collectives: 14.4 us -> none  [local_step(): peak_all = lax.pmax(row_peak, 'sp')]
    convert_element_type x2 -> x0, local copies, waits for them, and re-layouts: 4.55 us -> none  [the longest x1 2.39 us: local_step(): (value_all / weight_all[:, :, None]).astype(jnp.bfloat16)]
    reduce_sum x1 -> x0, other arithmetic: 3.01 us -> none  [local_step(): weight_sum = jnp.sum(weights, axis=2)]
  transfers between devices with their start and end apart: 1 -> 0, of which waited for: 1 -> 0; matrix products, arithmetic and copies ran while one was open for 0% -> 0% of each run, Pallas kernels for 0% -> 0%
where the time goes in v1:
time: 85.2 us; the launch traced here: 85.1 us
  Pallas kernels  83.6 us (98%)
    pallas_call x1, Pallas kernels, attention(): pl.pallas_call(functools.partial(attention_kernel, n_heads), out_shape=(j...  52.9 us
    pallas_call x1, Pallas kernels, combine(): pl.pallas_call(combine_kernel, out_shape=jax.ShapeDtypeStruct((n_rows, d_...  30.7 us

profile of v1, /device:TPU:0, one launch (start us, length us, event | category | flops | bytes accessed | tf_op | source)
XLA Modules:
  0.0 85.1 jit_solution(17171361846833470866)
XLA Ops:
  0.6 52.9 %attention.1 = (bf16[128,512,256]{2,1,0:T(8,128)(2,1)}, bf16[128,512,256]{2,1,0:T(8,128)(2,1)}, f32[4096,128]{1,0:T(8,128)S(1)}, f32[32,128]{1,0:T(8,128)S(1)}, bf16[640,2560]{1,0:T(8,128)(2,1)S(1)}) custom-call(s32[128]{0:T(128)} %pos_ref.1, bf16[128,2560]{1,0:T(8,128)(2,1)} %tok_hbm.1, bf16[2560,2560]{1,0:T(8,128)(2,1)} %wq_hbm.1, ...), custom_call_target="tpu_custom_call" | custom-call | flops 10000000000 | bytes 150000000 | tf_op jit(solution)/shard_map/attention/pallas_call | solution.py:144
  53.6 30.7 %combine.1 = bf16[128,2560]{1,0:T(8,128)(2,1)S(1)} custom-call(f32[4096,128]{1,0:T(8,128)S(1)} %get-tuple-element.8.o_ref, f32[32,128]{1,0:T(8,128)S(1)} %get-tuple-element.9.ml_ref, bf16[640,2560]{1,0:T(8,128)(2,1)S(1)} %get-tuple-element.10.wo), custom_call_target="tpu_custom_call" | custom-call | tf_op jit(solution)/shard_map/combine/pallas_call | solution.py:296
  84.2 0.8 copy.12

commit v2 on v0

v2 whole, which is shorter than its diff:
```python
import functools
import jax
import jax.numpy as jnp
from jax import lax
from jax.sharding import PartitionSpec as P
from jax.experimental import pallas as pl
from jax.experimental.pallas import tpu as pltpu

MESH = pl.DeviceIdType.MESH
F32 = jnp.float32
BF16 = jnp.bfloat16
HEAD_PAD = 16
BLOCK_ROWS = 8
COL_CHUNK = 512
PIECES = (16,) * 4
FIRST_ROWS = 128 - sum(PIECES)
GROUPS = (FIRST_ROWS, 32, 16, 16)
KINDS = ('quarter', 'quarter', 'quarter', 'half')
READ_AHEAD = 4
MIB = 1024 * 1024
ANY_SPEC = pl.BlockSpec(memory_space=pl.ANY)
VMEM_SPEC = pl.BlockSpec(memory_space=pltpu.VMEM)
SMEM_SPEC = pl.BlockSpec(memory_space=pltpu.SMEM)
DMA = pltpu.SemaphoreType.DMA


def patch_rows(buf, new, first, pos_ref, base, rows):
    seq_local, head_dim = buf.shape[-2:]
    sub = lax.broadcasted_iota(jnp.int32, (16, head_dim), 0)
    for i in rows:
        local = pos_ref[first + i] - base
        start = pl.multiple_of(jnp.clip(local // 16, 0, seq_local // 16 - 1) * 16, 16)
        tile = buf[i, pl.ds(start, 16), :].astype(F32)
        row = jnp.broadcast_to(new[pl.ds(first + i, 1), :], (16, head_dim))
        buf[i, pl.ds(start, 16), :] = jnp.where(sub == local - start, row, tile).astype(BF16)


def attend(first, pos_ref, base, scale, q_ref, kb, vb, s_scr, w_scr, o_ref, lane0, o_rows, carry, new=None):
    seq_local, head_dim = kb.shape[-2:]
    n_all = q_ref.shape[1] // HEAD_PAD
    half = head_dim // 2
    lane_t = lax.broadcasted_iota(jnp.int32, (HEAD_PAD, seq_local), 1)
    lane_b = lax.broadcasted_iota(jnp.int32, (HEAD_PAD, 128), 1)
    m_acc, l_acc = carry

    def query(b):
        return jnp.concatenate([q_ref[j, pl.ds(b, HEAD_PAD, stride=n_all), :] for j in range(2)], axis=1)

    for i in range(BLOCK_ROWS):
        s_scr[i] = lax.dot_general(query(first + i).astype(BF16), kb[i], (((1,), (1,)), ((), ())),
                                   preferred_element_type=F32)
    extra = []
    for i in range(BLOCK_ROWS):
        b = first + i
        local = pos_ref[b] - base
        s = s_scr[i]
        if new is not None:
            s_new = jnp.sum(query(b) * new[0][pl.ds(b, 1), :], axis=1, keepdims=True)
            s = jnp.where(lane_t == local, s_new, s)
        s = jnp.where(lane_t <= local, s * scale, -jnp.inf)
        m = jnp.maximum(jnp.max(s, axis=1, keepdims=True), -1e30)
        w = jnp.exp(s - m)
        l = jnp.sum(w, axis=1, keepdims=True)
        if new is not None:
            hit = lane_t == local
            extra.append(jnp.sum(jnp.where(hit, w, 0.0), axis=1, keepdims=True))
            w = jnp.where(hit, 0.0, w)
        w_scr[i] = w.astype(BF16)
        m_acc = jnp.where(lane_b == lane0 + i, m, m_acc)
        l_acc = jnp.where(lane_b == lane0 + i, l, l_acc)
    for i in range(BLOCK_ROWS):
        o = jnp.dot(w_scr[i], vb[i], preferred_element_type=F32)
        if new is not None:
            o = o + extra[i].astype(BF16).astype(F32) * new[1][pl.ds(first + i, 1), :]
        for j in range(2):
            o_ref[pl.ds(j * o_rows + lane0 + i, HEAD_PAD, stride=2 * o_rows), :] = o[:, j * half:(j + 1) * half]
    return m_acc, l_acc


def store_ml(ml_ref, carry):
    ml_ref[pl.ds(0, HEAD_PAD), :] = carry[0]
    ml_ref[pl.ds(HEAD_PAD, HEAD_PAD), :] = carry[1]


def zero_carry():
    return jnp.zeros((HEAD_PAD, 128), F32), jnp.zeros((HEAD_PAD, 128), F32)


def first_kernel(n_heads, pos_ref, tok_hbm, wq_hbm, wk_hbm, wv_hbm, k_hbm, v_hbm,
                 ko_hbm, vo_hbm, q_ref, kn_ref, vn_ref, o_ref, ml_ref,
                 tok, wq, wk, wv, s_scr, w_scr, kbuf, vbuf,
                 w_sems, wq_sems, kin_sems, vin_sems, kout_sems, vout_sems):
    n_rows, seq_local, head_dim = k_hbm.shape
    n_blocks = kbuf.shape[0]
    base = lax.axis_index('sp') * seq_local
    half = head_dim // 2

    def reads(blk):
        rows = pl.ds(blk * BLOCK_ROWS, BLOCK_ROWS)
        return (pltpu.make_async_copy(k_hbm.at[rows], kbuf.at[blk], kin_sems.at[blk]),
                pltpu.make_async_copy(v_hbm.at[rows], vbuf.at[blk], vin_sems.at[blk]))

    def writes(blk):
        rows = pl.ds(blk * BLOCK_ROWS, BLOCK_ROWS)
        return (pltpu.make_async_copy(kbuf.at[blk], ko_hbm.at[rows], kout_sems.at[blk]),
                pltpu.make_async_copy(vbuf.at[blk], vo_hbm.at[rows], vout_sems.at[blk]))

    small = [pltpu.make_async_copy(s, d, w_sems.at[i])
             for i, (s, d) in enumerate(((tok_hbm, tok), (wk_hbm, wk), (wv_hbm, wv)))]
    n_chunks = wq.shape[1] // COL_CHUNK
    big = [pltpu.make_async_copy(wq_hbm.at[:, pl.ds(i * COL_CHUNK, COL_CHUNK)],
                                 wq.at[:, pl.ds(i * COL_CHUNK, COL_CHUNK)], wq_sems.at[i])
           for i in range(n_chunks)]
    for c in small + big:
        c.start()
    for c in reads(0):
        c.start()
    for j in range(2):
        q_ref[j, pl.ds(n_heads * n_rows, (HEAD_PAD - n_heads) * n_rows), :] = jnp.zeros(
            ((HEAD_PAD - n_heads) * n_rows, half), F32)
    for c in small:
        c.wait()

    def project(w):
        return jnp.dot(tok[...], w, preferred_element_type=F32).astype(BF16).astype(F32)

    kn_ref[...] = project(wk[...])
    vn_ref[...] = project(wv[...])
    per_chunk = COL_CHUNK // head_dim

    def pass_through(blk):
        for c in reads(blk):
            c.wait()
        patch_rows(kbuf.at[blk], kn_ref, blk * BLOCK_ROWS, pos_ref, base, range(BLOCK_ROWS))
        patch_rows(vbuf.at[blk], vn_ref, blk * BLOCK_ROWS, pos_ref, base, range(BLOCK_ROWS))
        for c in writes(blk):
            c.start()

    for i in range(n_chunks):
        if i + 1 < n_blocks:
            for c in reads(i + 1):
                c.start()
        big[i].wait()
        for h in range(i * per_chunk, (i + 1) * per_chunk):
            q_head = project(wq[:, pl.ds(h * head_dim, head_dim)])
            for j in range(2):
                q_ref[j, pl.ds(h * n_rows, n_rows), :] = q_head[:, j * half:(j + 1) * half]
    for blk in range(n_chunks + 1, n_blocks):
        for c in reads(blk):
            c.start()

    def block(blk, carry):
        pass_through(blk)
        return attend(blk * BLOCK_ROWS, pos_ref, base, head_dim ** -0.5, q_ref, kbuf.at[blk], vbuf.at[blk],
                      s_scr, w_scr, o_ref, blk * BLOCK_ROWS, n_blocks * BLOCK_ROWS, carry)

    store_ml(ml_ref, lax.fori_loop(0, n_blocks, block, zero_carry()))
    for blk in range(n_blocks):
        for c in writes(blk):
            c.wait()


def first_part(pos, tok, wq, wk, wv, k, v):
    n_rows, seq_local, head_dim = k.shape
    d_model, q_width = wq.shape
    n_heads = q_width // head_dim
    n_blocks = FIRST_ROWS // BLOCK_ROWS
    block = pltpu.VMEM((n_blocks, BLOCK_ROWS, seq_local, head_dim), BF16)
    return pl.pallas_call(
        functools.partial(first_kernel, n_heads),
        out_shape=(jax.ShapeDtypeStruct(k.shape, k.dtype), jax.ShapeDtypeStruct(v.shape, v.dtype),
                   pltpu.VMEM((2, HEAD_PAD * n_rows, head_dim // 2), F32),
                   pltpu.VMEM((n_rows, head_dim), F32), pltpu.VMEM((n_rows, head_dim), F32),
                   pltpu.VMEM((2 * HEAD_PAD * FIRST_ROWS, head_dim // 2), F32),
                   pltpu.VMEM((2 * HEAD_PAD, 128), F32)),
        in_specs=[SMEM_SPEC] + [ANY_SPEC] * 6,
        out_specs=(ANY_SPEC, ANY_SPEC) + (VMEM_SPEC,) * 5,
        scratch_shapes=[
            pltpu.VMEM(tok.shape, BF16), pltpu.VMEM(wq.shape, BF16),
            pltpu.VMEM(wk.shape, BF16), pltpu.VMEM(wv.shape, BF16),
            pltpu.VMEM((BLOCK_ROWS, HEAD_PAD, seq_local), F32),
            pltpu.VMEM((BLOCK_ROWS, HEAD_PAD, seq_local), BF16),
            block, block,
            DMA((3,)), DMA((q_width // COL_CHUNK,)),
            DMA((n_blocks,)), DMA((n_blocks,)), DMA((n_blocks,)), DMA((n_blocks,))],
        compiler_params=pltpu.CompilerParams(vmem_limit_bytes=60 * MIB),
        cost_estimate=pl.CostEstimate(flops=10**10, bytes_accessed=70 * 10**6, transcendentals=0),
        name='attention_first',
    )(pos, tok, wq, wk, wv, k, v)


COPIES = 10
N_PIECES = len(PIECES)
PIECE_ROW0 = tuple(sum(PIECES[:i]) for i in range(N_PIECES))


class Group:
    def __init__(self):
        self.copies = {}

    def __getattr__(self, name):
        return self.__dict__['copies'][name]()


def rest_kernel(pos_ref, q_ref, kn_ref, vn_ref, o0, ml0, wo_hbm, k_hbm, v_hbm,
                *refs):
    kret, vret = refs[:N_PIECES], refs[N_PIECES:2 * N_PIECES]
    rest_body(pos_ref, q_ref, kn_ref, vn_ref, o0, ml0, wo_hbm, k_hbm, v_hbm, kret, vret, *refs[2 * N_PIECES:])


def rest_body(pos_ref, q_ref, kn_ref, vn_ref, o0, ml0, wo_hbm, k_hbm, v_hbm,
              kret, vret, y_ref, wo, s_scr, w_scr, fbuf, wo_sem, kin_sems, vin_sems, send, recv, *scratch):
    n_rows, seq_local, head_dim = k_hbm.shape
    rows_local, d_model = wo.shape
    units = rows_local // 128
    half_width = d_model // 2
    n_blocks = sum(PIECES) // BLOCK_ROWS
    me = lax.axis_index('sp')
    base = me * seq_local
    core = lax.rem(me, 2)
    chip = me // 2
    partner = chip * 2 + 1 - core
    cross = (1 - chip) * 2 + core
    far, near = (1 - chip) * 2, chip * 2

    def reads(blk):
        p = piece_of(blk)
        src = pl.ds(FIRST_ROWS + blk * BLOCK_ROWS, BLOCK_ROWS)
        dst = pl.ds(blk * BLOCK_ROWS - PIECE_ROW0[p], BLOCK_ROWS)
        return (pltpu.make_async_copy(k_hbm.at[src], kret[p].at[dst], kin_sems.at[blk]),
                pltpu.make_async_copy(v_hbm.at[src], vret[p].at[dst], vin_sems.at[blk]))

    barrier = pltpu.get_barrier_semaphore()
    for peer in (partner, cross):
        pl.semaphore_signal(barrier, inc=1, device_id={'sp': peer}, device_id_type=MESH)
    for blk in range(min(READ_AHEAD, n_blocks)):
        for c in reads(blk):
            c.start()
    load_wo = pltpu.make_async_copy(wo_hbm, wo, wo_sem)
    load_wo.start()

    def group(idx):
        g = Group()
        g.n, g.row0 = GROUPS[idx], sum(GROUPS[:idx])
        refs = scratch[idx * len(BUFS):(idx + 1) * len(BUFS)]
        for name, ref in zip(BUFS, refs):
            setattr(g, name, ref)
        if idx == 0:
            g.o, g.ml = o0, ml0
        g.span = units * g.n

        def remote(i, src, dst, peer):
            return pltpu.make_async_remote_copy(src_ref=src, dst_ref=dst, send_sem=send.at[idx, i],
                                                recv_sem=recv.at[idx, i], device_id={'sp': peer},
                                                device_id_type=MESH)

        def part(dest):
            return g.o.at[pl.ds(pl.multiple_of(dest * g.span, 8), g.span)]

        g.copies['p_ml'] = lambda: remote(0, g.ml, g.pml, partner)
        g.copies['p_far'] = lambda: remote(1, part(far + 1 - core), g.po.at[0], partner)
        g.copies['p_near'] = lambda: remote(2, part(near + 1 - core), g.po.at[1], partner)
        g.copies['x_ml'] = lambda: remote(3, g.mlc, g.xml, cross)
        g.copies['x_o'] = lambda: remote(4, g.oc, g.xo, cross)
        g.copies['p_y'] = lambda: remote(5, g.yq, g.yp, partner)
        g.copies['x_y'] = lambda: remote(6, g.yx, g.yxr, cross)
        if KINDS[idx] == 'half':
            g.copies['p_b'] = lambda: remote(7, g.yb, g.yg, partner)
        else:
            g.copies['p_b'] = lambda: remote(7, g.yb, g.yg.at[1], partner)
            g.copies['x_b'] = lambda: remote(8, g.yb, g.yg.at[0], cross)
            g.copies['p_f'] = lambda: remote(9, g.yg.at[0], g.yg.at[2], partner)
        return g

    def merge(a, b):
        peak = jnp.maximum(a[:HEAD_PAD], b[:HEAD_PAD])
        fa = jnp.exp(a[:HEAD_PAD] - peak)
        fb = jnp.exp(b[:HEAD_PAD] - peak)
        return fa, fb, peak, a[HEAD_PAD:] * fa + b[HEAD_PAD:] * fb

    def columns(k, dest, n):
        picks = [fbuf[k, pl.ds((dest * units + u) // 2, 1), :] for u in range(units)]
        picks += [picks[-1]] * (8 - units)
        return jnp.concatenate(picks, axis=0).T[:n]

    def stage0(g):
        for c in (g.p_ml, g.p_far, g.p_near):
            c.start()

    def stage1(g):
        g.p_ml.wait_recv()
        fa, fb, peak, total = merge(g.ml[...], g.pml[...])
        fbuf[0] = fa
        fbuf[1] = fb
        g.mlc[pl.ds(0, HEAD_PAD), :] = peak
        g.mlc[pl.ds(HEAD_PAD, HEAD_PAD), :] = total
        g.x_ml.start()

        def chip_part(dest, slot, dst):
            ca, cb = columns(0, dest, g.n), columns(1, dest, g.n)
            for u in range(units):
                mine = g.o[pl.ds(pl.multiple_of(dest * g.span + u * g.n, 8), g.n), :]
                theirs = g.po[slot, pl.ds(u * g.n, g.n), :]
                dst[pl.ds(u * g.n, g.n), :] = mine * ca[:, u:u + 1] + theirs * cb[:, u:u + 1]

        g.p_far.wait_recv()
        chip_part(far + core, 0, g.oc)
        g.x_o.start()
        g.p_near.wait_recv()
        chip_part(me, 1, g.om)

    def stage2(g):
        g.x_ml.wait_recv()
        fa, fb, peak, total = merge(g.mlc[...], g.xml[...])
        fbuf[2] = fa
        fbuf[3] = fb
        fbuf[4] = total
        ca, cb, cl = columns(2, me, g.n), columns(3, me, g.n), columns(4, me, g.n)
        g.x_o.wait_recv()
        for u in range(units):
            rows = pl.ds(u * g.n, g.n)
            value = g.om[rows, :] * ca[:, u:u + 1] + g.xo[rows, :] * cb[:, u:u + 1]
            g.ob[:, u * 128:(u + 1) * 128] = (value / cl[:, u:u + 1]).astype(BF16)

        def product(c):
            cols = pl.ds(pl.multiple_of(c * half_width, 128), half_width)
            return jnp.dot(g.ob[...], wo[:, cols], preferred_element_type=F32)

        g.yq[...] = product(1 - core)
        g.p_y.start()
        g.ym[...] = product(core)

    def place(g, start, value):
        width = value.shape[1]
        y_ref[pl.ds(g.row0, g.n), pl.ds(pl.multiple_of(start, 128), width)] = value

    def stage3_half(g):
        g.p_y.wait_recv()
        g.yx[...] = g.ym[...] + g.yp[...]
        g.x_y.start()

    def stage4_half(g):
        g.x_y.wait_recv()
        g.yb[...] = (g.yx[...] + g.yxr[...]).astype(BF16)
        g.p_b.start()
        place(g, core * half_width, g.yb[...])

    def finish(g):
        for name in g.copies:
            g.copies[name]().wait_send()

    def stage5_half(g):
        g.p_b.wait_recv()
        place(g, (1 - core) * half_width, g.yg[...])
        finish(g)

    quarter = half_width // 2
    far_cols = pl.ds(pl.multiple_of((1 - chip) * quarter, 128), quarter)
    near_cols = pl.ds(pl.multiple_of(chip * quarter, 128), quarter)

    def stage3_quarter(g):
        g.p_y.wait_recv()
        g.yx[...] = g.ym[:, far_cols] + g.yp[:, far_cols]
        g.x_y.start()
        g.yn[...] = g.ym[:, near_cols] + g.yp[:, near_cols]

    def stage4_quarter(g):
        g.x_y.wait_recv()
        g.yb[...] = (g.yn[...] + g.yxr[...]).astype(BF16)
        g.x_b.start()
        g.p_b.start()
        place(g, core * half_width + chip * quarter, g.yb[...])

    def stage5_quarter(g):
        g.x_b.wait_recv()
        g.p_f.start()
        place(g, core * half_width + (1 - chip) * quarter, g.yg[0])

    def stage6_quarter(g):
        g.p_b.wait_recv()
        place(g, (1 - core) * half_width + chip * quarter, g.yg[1])
        g.p_f.wait_recv()
        place(g, (1 - core) * half_width + (1 - chip) * quarter, g.yg[2])
        finish(g)

    common = (stage0, stage1, stage2)
    stages = dict(half=common + (stage3_half, stage4_half, stage5_half),
                  quarter=common + (stage3_quarter, stage4_quarter, stage5_quarter, stage6_quarter))
    groups = [group(i) for i in range(len(GROUPS))]

    def attend_block(blk):
        if blk + READ_AHEAD < n_blocks:
            for c in reads(blk + READ_AHEAD):
                c.start()
        for c in reads(blk):
            c.wait()
        p = piece_of(blk)
        row = FIRST_ROWS + blk * BLOCK_ROWS
        idx = [i for i in range(len(GROUPS)) if row >= sum(GROUPS[:i])][-1]
        g = groups[idx]
        lane0 = row - g.row0
        carry = zero_carry() if lane0 == 0 else (g.ml[pl.ds(0, HEAD_PAD), :], g.ml[pl.ds(HEAD_PAD, HEAD_PAD), :])
        rows = pl.ds(blk * BLOCK_ROWS - PIECE_ROW0[p], BLOCK_ROWS)
        store_ml(g.ml, attend(row, pos_ref, base, head_dim ** -0.5, q_ref, kret[p].at[rows], vret[p].at[rows],
                              s_scr, w_scr, g.o, lane0, g.n, carry, (kn_ref, vn_ref)))

    for action in SCHEDULE:
        if isinstance(action, int):
            attend_block(action)
        elif action == 'wo':
            load_wo.wait()
        elif action == 'barrier':
            pl.semaphore_wait(barrier, 2)
        else:
            stages[KINDS[action[0]]][action[1]](groups[action[0]])


def piece_of(blk):
    return [i for i in range(N_PIECES) if blk * BLOCK_ROWS >= PIECE_ROW0[i]][-1]


BUFS = ('o', 'ml', 'pml', 'po', 'mlc', 'oc', 'om', 'xo', 'xml', 'ob', 'yq', 'yp', 'ym', 'yn', 'yx', 'yxr', 'yb',
        'yg')
SCHEDULE = ('barrier', (0, 0), 0, (0, 1), 1, 2, 3, (1, 0), 4, (1, 1), 5, (2, 0), 'wo', (0, 2), (2, 1), 6, (0,
            3), 7, (3, 0), (1, 2), (3, 1), (2, 2), (1, 3), (2, 3), (0, 4), (3, 2), (1, 4), (3, 3), (2, 4), (0,
            5), (1, 5), (0, 6), (1, 6), (3, 4), (2, 5), (3, 5), (2, 6))


def rest_part(pos, q, kn, vn, o0, ml0, wo, k, v):
    n_rows, seq_local, head_dim = k.shape
    rows_local, d_model = wo.shape
    units = rows_local // 128
    n_blocks = sum(PIECES) // BLOCK_ROWS

    def buffers(n, own, kind):
        span = units * n
        ml, part, half = (2 * HEAD_PAD, 128), (span, 128), (n, d_model // 2)
        slab = half if kind == 'half' else (n, d_model // 4)
        shapes = dict(o=((2 * HEAD_PAD * n if own else 8, 128), F32), ml=(ml, F32),
                      pml=(ml, F32), po=((2,) + part, F32), mlc=(ml, F32), oc=(part, F32), om=(part, F32),
                      xo=(part, F32), xml=(ml, F32), ob=((n, rows_local), BF16), yq=(half, F32), yp=(half, F32),
                      ym=(half, F32), yn=(slab if kind != 'half' else (8, 128), F32), yx=(slab, F32),
                      yxr=(slab, F32), yb=(slab, BF16), yg=(slab if kind == 'half' else (3,) + slab, BF16))
        return [pltpu.VMEM(*shapes[name]) for name in BUFS]

    return pl.pallas_call(
        rest_kernel,
        out_shape=tuple(pltpu.VMEM((n, seq_local, head_dim), BF16) for n in PIECES * 2)
        + (pltpu.VMEM((n_rows, d_model), BF16),),
        in_specs=[SMEM_SPEC] + [VMEM_SPEC] * 5 + [ANY_SPEC] * 3,
        out_specs=(VMEM_SPEC,) * (2 * N_PIECES + 1),
        scratch_shapes=[
            pltpu.VMEM(wo.shape, BF16),
            pltpu.VMEM((BLOCK_ROWS, HEAD_PAD, seq_local), F32),
            pltpu.VMEM((BLOCK_ROWS, HEAD_PAD, seq_local), BF16),
            pltpu.VMEM((5, HEAD_PAD, 128), F32),
            DMA, DMA((n_blocks,)), DMA((n_blocks,)), DMA((len(GROUPS), COPIES)), DMA((len(GROUPS), COPIES))]
            + [b for i, n in enumerate(GROUPS) for b in buffers(n, i > 0, KINDS[i])],
        compiler_params=pltpu.CompilerParams(collective_id=0, has_side_effects=True, vmem_limit_bytes=REST_VMEM * MIB),
        cost_estimate=pl.CostEstimate(flops=10**10, bytes_accessed=40 * 10**6, transcendentals=0),
        name='attention_rest',
    )(pos, q, kn, vn, o0, ml0, wo, k, v)


REST_VMEM = 18


def write_kernel(pos_ref, kn_ref, vn_ref, y_ref, *refs):
    ko_hbm, vo_hbm, y_hbm = refs[2 * N_PIECES + 2:2 * N_PIECES + 5]
    kret, vret = refs[2 * N_PIECES + 5:3 * N_PIECES + 5], refs[3 * N_PIECES + 5:4 * N_PIECES + 5]
    k_sems, v_sems, y_sem = refs[4 * N_PIECES + 5:]
    seq_local = ko_hbm.shape[1]
    n_blocks = sum(PIECES) // BLOCK_ROWS
    base = lax.axis_index('sp') * seq_local
    write_y = pltpu.make_async_copy(y_ref, y_hbm, y_sem)

    def writes(blk):
        p = piece_of(blk)
        src = pl.ds(blk * BLOCK_ROWS - PIECE_ROW0[p], BLOCK_ROWS)
        dst = pl.ds(FIRST_ROWS + blk * BLOCK_ROWS, BLOCK_ROWS)
        return (pltpu.make_async_copy(kret[p].at[src], ko_hbm.at[dst], k_sems.at[blk]),
                pltpu.make_async_copy(vret[p].at[src], vo_hbm.at[dst], v_sems.at[blk]))

    for blk in range(n_blocks):
        p = piece_of(blk)
        rows = pl.ds(blk * BLOCK_ROWS - PIECE_ROW0[p], BLOCK_ROWS)
        for kept, new, copy in zip((kret, vret), (kn_ref, vn_ref), writes(blk)):
            patch_rows(kept[p].at[rows], new, FIRST_ROWS + blk * BLOCK_ROWS, pos_ref, base, range(BLOCK_ROWS))
            copy.start()
    write_y.start()
    write_y.wait()
    for blk in range(n_blocks):
        for c in writes(blk):
            c.wait()


def write_part(pos, kn, vn, y, ko, vo, kret, vret):
    n_blocks = sum(PIECES) // BLOCK_ROWS
    kept = (*kret, *vret)
    out = pl.pallas_call(
        write_kernel,
        out_shape=(jax.ShapeDtypeStruct(ko.shape, ko.dtype), jax.ShapeDtypeStruct(vo.shape, vo.dtype),
                   jax.ShapeDtypeStruct(y.shape, y.dtype)) + tuple(pltpu.VMEM(a.shape, a.dtype) for a in kept),
        in_specs=[SMEM_SPEC, VMEM_SPEC, VMEM_SPEC, VMEM_SPEC] + [VMEM_SPEC] * (2 * N_PIECES) + [ANY_SPEC, ANY_SPEC],
        out_specs=(ANY_SPEC, ANY_SPEC, ANY_SPEC) + (VMEM_SPEC,) * (2 * N_PIECES),
        input_output_aliases={4 + 2 * N_PIECES: 0, 5 + 2 * N_PIECES: 1,
                              **{4 + i: 3 + i for i in range(2 * N_PIECES)}},
        scratch_shapes=[DMA((n_blocks,)), DMA((n_blocks,)), DMA],
        compiler_params=pltpu.CompilerParams(vmem_limit_bytes=REST_VMEM * MIB),
        cost_estimate=pl.CostEstimate(flops=10**10, bytes_accessed=40 * 10**6, transcendentals=0),
        name='attention_write',
    )(pos, kn, vn, y, *kept, ko, vo)
    return out[2], out[0], out[1]


def in_vmem(*arrays):
    return [pltpu.with_memory_space_constraint(a, pltpu.VMEM) for a in arrays]


def solution(mesh):
    def local_step(tokens, w_query, w_key, w_value, w_out, k_cache, v_cache, positions):
        ko, vo, q, kn, vn, o0, ml0 = first_part(
            positions, tokens, w_query, w_key, w_value, k_cache, v_cache)
        q, kn, vn, o0, ml0 = in_vmem(q, kn, vn, o0, ml0)
        *kept, y = rest_part(positions, q, kn, vn, o0, ml0, w_out, k_cache, v_cache)
        *kept, y = in_vmem(*kept, y)
        return write_part(positions, kn, vn, y, ko, vo, kept[:N_PIECES], kept[N_PIECES:])

    cache_spec = P('dp', 'sp', None)
    return jax.shard_map(local_step, mesh=mesh, in_specs=(P('dp', None), P(), P(), P(), P('sp', None), cache_spec, cache_spec, P('dp')), out_specs=(P('dp', None), cache_spec, cache_spec), check_vma=False)
```

time: 212 us -> 72.4 us (0.34)
  Pallas kernels: 0 us -> 71.7 us
  blocking collectives: 54.9 us -> 0 us
  other arithmetic: 51.9 us -> 0 us
  matrix products: 49.2 us -> 0 us
  waiting for transfers between devices: 34.6 us -> 0 us
  between operations: 14.1 us -> 0.66 us
  local copies, waits for them, and re-layouts: 7.16 us -> 0.01 us
    pallas_call x0 -> x3, Pallas kernels: none -> 71.7 us  [the longest x1 31.6 us: rest_part(): pl.pallas_call(rest_kernel, out_shape=tuple((pltpu.VMEM((n, seq_local, he...]
    dot_general x6 -> x0, matrix products: 49.2 us -> none  [the longest x1 18.2 us: local_step(): jnp.einsum('bht,btd->bhd', weights.astype(jnp.bfloat16), v_upd, preferred...]
    select_n x1 -> x0, other arithmetic: 44.5 us -> none  [local_step(): k_upd = jnp.where(hit_mask, key_new[:, None, :], k_cache)]
    psum x2 -> x0, blocking collectives: 40.5 us -> none  [the longest x1 28.4 us: local_step(): attn_out = lax.psum(partial, 'sp').astype(jnp.bfloat16)]
    psum x1 -> x0, waiting for transfers between devices: 34.5 us -> none  [local_step(): value_all = lax.psum(value_sum * rescale[:, :, None], 'sp')]
    pmax x1 -> x0, blocking collectives: 14.4 us -> none  [local_step(): peak_all = lax.pmax(row_peak, 'sp')]
    convert_element_type x2 -> x0, local copies, waits for them, and re-layouts: 4.55 us -> none  [the longest x1 2.39 us: local_step(): (value_all / weight_all[:, :, None]).astype(jnp.bfloat16)]
    reduce_sum x1 -> x0, other arithmetic: 3.01 us -> none  [local_step(): weight_sum = jnp.sum(weights, axis=2)]
  transfers between devices with their start and end apart: 1 -> 0, of which waited for: 1 -> 0; matrix products, arithmetic and copies ran while one was open for 0% -> 0% of each run, Pallas kernels for 0% -> 0%
where the time goes in v2:
time: 72.4 us; the launch traced here: 72.3 us
  Pallas kernels  71.7 us (99%)
    pallas_call x1, Pallas kernels, rest_part(): pl.pallas_call(rest_kernel, out_shape=tuple((pltpu.VMEM((n, seq_local, he...  31.6 us
    pallas_call x1, Pallas kernels, first_part(): pl.pallas_call(functools.partial(first_kernel, n_heads), out_shape=(jax.S...  28.2 us
    pallas_call x1, Pallas kernels, write_part(): pl.pallas_call(write_kernel, out_shape=(jax.ShapeDtypeStruct(ko.shape, ko...  11.9 us

profile of v2, /device:TPU:0, one launch (start us, length us, event | category | flops | bytes accessed | tf_op | source)
XLA Modules:
  0.0 72.3 jit_solution(739103773699764287)
XLA Ops:
  0.6 0.0 copy-start
  0.6 28.2 %attention_first.1 = (bf16[128,512,256]{2,1,0:T(8,128)(2,1)}, bf16[128,512,256]{2,1,0:T(8,128)(2,1)}, f32[2,2048,128]{2,1,0:T(8,128)S(1)}, f32[128,256]{1,0:T(8,...) custom-call(s32[128]{0:T(128)} %pos_ref.5, bf16[128,2560]{1,0:T(8,128)(2,1)} %tok_hbm.1, ...), custom_call_target="tpu_custom_call" | custom-call | flops 10000000000 | bytes 70000000 | tf_op jit(solution)/shard_map/attention_first/pallas_call | solution.py:169
  28.8 0.0 copy-done
  28.9 31.6 %attention_rest.1 = (bf16[16,512,256]{2,1,0:T(8,128)(2,1)S(1)}, bf16[16,512,256]{2,1,0:T(8,128)(2,1)S(1)}, bf16[16,512,256]{2,1,0:T(8,128)(2,1)S(1)}, bf16[16,51...) custom-call(s32[128]{0:T(128)S(1)} %copy-done, ...), custom_call_target="tpu_custom_call" | custom-call | flops 10000000000 | bytes 40000000 | tf_op jit(solution)/shard_map/attention_rest/pallas_call | solution.py:446
  60.5 11.9 %attention_write.1 = (bf16[128,512,256]{2,1,0:T(8,128)(2,1)}, bf16[128,512,256]{2,1,0:T(8,128)(2,1)}, bf16[128,2560]{1,0:T(8,128)(2,1)}, bf16[16,512,256]{2,1,0:...) custom-call(s32[128]{0:T(128)S(1)} %copy-done, ...), custom_call_target="tpu_custom_call", output_to_operand_aliasing={{0}: (12, {}), {1}: (13, {}), {3}: (4, {}), {4}: (5, {}), {... | custom-call | flops 10000000000 | bytes 40000000 | tf_op jit(solution)/shard_map/attention_write/pallas_call | solution.py:500
Async XLA Ops:
  0.6 28.2 %copy-start = (s32[128]{0:T(128)S(1)}, s32[128]{0:T(128)}, u32[]{:S(2)}) copy-start(s32[128]{0:T(128)} %pos_ref.5) | copy-start | bytes 1540

commit v3 on v2

--- a/solution.py
+++ b/solution.py
@@ -11,12 +11,14 @@
 BF16 = jnp.bfloat16
 HEAD_PAD = 16
 BLOCK_ROWS = 8
+DMA_ROWS = 16
+EARLY = 2
 COL_CHUNK = 512
 PIECES = (16,) * 4
 FIRST_ROWS = 128 - sum(PIECES)
-GROUPS = (FIRST_ROWS, 32, 16, 16)
+GROUPS = (FIRST_ROWS, 24, 24, 16)
 KINDS = ('quarter', 'quarter', 'quarter', 'half')
-READ_AHEAD = 4
+READ_AHEAD = 6
 MIB = 1024 * 1024
 ANY_SPEC = pl.BlockSpec(memory_space=pl.ANY)
 VMEM_SPEC = pl.BlockSpec(memory_space=pltpu.VMEM)
@@ -96,12 +98,12 @@
     half = head_dim // 2
 
     def reads(blk):
-        rows = pl.ds(blk * BLOCK_ROWS, BLOCK_ROWS)
+        rows = pl.ds(blk * DMA_ROWS, DMA_ROWS)
         return (pltpu.make_async_copy(k_hbm.at[rows], kbuf.at[blk], kin_sems.at[blk]),
                 pltpu.make_async_copy(v_hbm.at[rows], vbuf.at[blk], vin_sems.at[blk]))
 
     def writes(blk):
-        rows = pl.ds(blk * BLOCK_ROWS, BLOCK_ROWS)
+        rows = pl.ds(blk * DMA_ROWS, DMA_ROWS)
         return (pltpu.make_async_copy(kbuf.at[blk], ko_hbm.at[rows], kout_sems.at[blk]),
                 pltpu.make_async_copy(vbuf.at[blk], vo_hbm.at[rows], vout_sems.at[blk]))
 
@@ -128,13 +130,11 @@
     vn_ref[...] = project(wv[...])
     per_chunk = COL_CHUNK // head_dim
 
-    def pass_through(blk):
+    def arrive(blk):
         for c in reads(blk):
             c.wait()
-        patch_rows(kbuf.at[blk], kn_ref, blk * BLOCK_ROWS, pos_ref, base, range(BLOCK_ROWS))
-        patch_rows(vbuf.at[blk], vn_ref, blk * BLOCK_ROWS, pos_ref, base, range(BLOCK_ROWS))
-        for c in writes(blk):
-            c.start()
+        patch_rows(kbuf.at[blk], kn_ref, blk * DMA_ROWS, pos_ref, base, range(DMA_ROWS))
+        patch_rows(vbuf.at[blk], vn_ref, blk * DMA_ROWS, pos_ref, base, range(DMA_ROWS))
 
     for i in range(n_chunks):
         if i + 1 < n_blocks:
@@ -150,11 +150,24 @@
             c.start()
 
     def block(blk, carry):
-        pass_through(blk)
-        return attend(blk * BLOCK_ROWS, pos_ref, base, head_dim ** -0.5, q_ref, kbuf.at[blk], vbuf.at[blk],
-                      s_scr, w_scr, o_ref, blk * BLOCK_ROWS, n_blocks * BLOCK_ROWS, carry)
-
-    store_ml(ml_ref, lax.fori_loop(0, n_blocks, block, zero_carry()))
+        for j in range(DMA_ROWS // BLOCK_ROWS):
+            first = blk * DMA_ROWS + j * BLOCK_ROWS
+            rows = pl.ds(j * BLOCK_ROWS, BLOCK_ROWS)
+            carry = attend(first, pos_ref, base, head_dim ** -0.5, q_ref, kbuf.at[blk, rows], vbuf.at[blk, rows],
+                           s_scr, w_scr, o_ref, first, n_blocks * DMA_ROWS, carry)
+        return carry
+
+    def early_block(blk, carry):
+        arrive(blk)
+        return block(blk, carry)
+
+    carry = lax.fori_loop(0, EARLY, early_block, zero_carry())
+    for blk in range(EARLY, n_blocks):
+        arrive(blk)
+    for blk in range(n_blocks):
+        for c in writes(blk):
+            c.start()
+    store_ml(ml_ref, lax.fori_loop(EARLY, n_blocks, block, carry))
     for blk in range(n_blocks):
         for c in writes(blk):
             c.wait()
@@ -164,8 +177,8 @@
     n_rows, seq_local, head_dim = k.shape
     d_model, q_width = wq.shape
     n_heads = q_width // head_dim
-    n_blocks = FIRST_ROWS // BLOCK_ROWS
-    block = pltpu.VMEM((n_blocks, BLOCK_ROWS, seq_local, head_dim), BF16)
+    n_blocks = FIRST_ROWS // DMA_ROWS
+    block = pltpu.VMEM((n_blocks, DMA_ROWS, seq_local, head_dim), BF16)
     return pl.pallas_call(
         functools.partial(first_kernel, n_heads),
         out_shape=(jax.ShapeDtypeStruct(k.shape, k.dtype), jax.ShapeDtypeStruct(v.shape, v.dtype),
@@ -273,15 +286,15 @@
         return g
 
     def merge(a, b):
-        peak = jnp.maximum(a[:HEAD_PAD], b[:HEAD_PAD])
-        fa = jnp.exp(a[:HEAD_PAD] - peak)
-        fb = jnp.exp(b[:HEAD_PAD] - peak)
-        return fa, fb, peak, a[HEAD_PAD:] * fa + b[HEAD_PAD:] * fb
-
-    def columns(k, dest, n):
-        picks = [fbuf[k, pl.ds((dest * units + u) // 2, 1), :] for u in range(units)]
-        picks += [picks[-1]] * (8 - units)
-        return jnp.concatenate(picks, axis=0).T[:n]
+        n = a.shape[0] // 2
+        peak = jnp.maximum(a[:n], b[:n])
+        fa = jnp.exp(a[:n] - peak)
+        fb = jnp.exp(b[:n] - peak)
+        return fa, fb, peak, a[n:] * fa + b[n:] * fb
+
+    def picks(k, dest):
+        rows = [fbuf[k, pl.ds((dest * units + u) // 2, 1), :] for u in range(units)]
+        return jnp.concatenate(rows + [rows[-1]] * (8 - units), axis=0)
 
     def stage0(g):
         for c in (g.p_ml, g.p_far, g.p_near):
@@ -289,15 +302,15 @@
 
     def stage1(g):
         g.p_ml.wait_recv()
-        fa, fb, peak, total = merge(g.ml[...], g.pml[...])
-        fbuf[0] = fa
-        fbuf[1] = fb
-        g.mlc[pl.ds(0, HEAD_PAD), :] = peak
-        g.mlc[pl.ds(HEAD_PAD, HEAD_PAD), :] = total
+        for k, value in enumerate(merge(g.ml[...], g.pml[...])):
+            fbuf[k] = value
+        for ref, dest in ((g.mlc, far + core), (g.mlo, me)):
+            ref[pl.ds(0, 8), :] = picks(2, dest)
+            ref[pl.ds(8, 8), :] = picks(3, dest)
         g.x_ml.start()
 
         def chip_part(dest, slot, dst):
-            ca, cb = columns(0, dest, g.n), columns(1, dest, g.n)
+            ca, cb = picks(0, dest).T[:g.n], picks(1, dest).T[:g.n]
             for u in range(units):
                 mine = g.o[pl.ds(pl.multiple_of(dest * g.span + u * g.n, 8), g.n), :]
                 theirs = g.po[slot, pl.ds(u * g.n, g.n), :]
@@ -311,11 +324,8 @@
 
     def stage2(g):
         g.x_ml.wait_recv()
-        fa, fb, peak, total = merge(g.mlc[...], g.xml[...])
-        fbuf[2] = fa
-        fbuf[3] = fb
-        fbuf[4] = total
-        ca, cb, cl = columns(2, me, g.n), columns(3, me, g.n), columns(4, me, g.n)
+        fa, fb, _, total = merge(g.mlo[...], g.xml[...])
+        ca, cb, cl = fa.T[:g.n], fb.T[:g.n], total.T[:g.n]
         g.x_o.wait_recv()
         for u in range(units):
             rows = pl.ds(u * g.n, g.n)
@@ -419,11 +429,11 @@
     return [i for i in range(N_PIECES) if blk * BLOCK_ROWS >= PIECE_ROW0[i]][-1]
 
 
-BUFS = ('o', 'ml', 'pml', 'po', 'mlc', 'oc', 'om', 'xo', 'xml', 'ob', 'yq', 'yp', 'ym', 'yn', 'yx', 'yxr', 'yb',
+BUFS = ('o', 'ml', 'pml', 'po', 'mlc', 'mlo', 'oc', 'om', 'xo', 'xml', 'ob', 'yq', 'yp', 'ym', 'yn', 'yx', 'yxr', 'yb',
         'yg')
-SCHEDULE = ('barrier', (0, 0), 0, (0, 1), 1, 2, 3, (1, 0), 4, (1, 1), 5, (2, 0), 'wo', (0, 2), (2, 1), 6, (0,
-            3), 7, (3, 0), (1, 2), (3, 1), (2, 2), (1, 3), (2, 3), (0, 4), (3, 2), (1, 4), (3, 3), (2, 4), (0,
-            5), (1, 5), (0, 6), (1, 6), (3, 4), (2, 5), (3, 5), (2, 6))
+SCHEDULE = ('barrier', (0, 0), 0, (0, 1), 1, 2, (1, 0), 3, (1, 1), 4, 5, (2, 0), 'wo', (0, 2), (2, 1), 6, (0,
+            3), 7, (3, 0), (1, 2), (3, 1), (2, 2), (1, 3), (2, 3), (0, 4), (3, 2), (1, 4), (3, 3), (2, 4), (1,
+            5), (1, 6), (0, 5), (3, 4), (2, 5), (3, 5), (0, 6), (2, 6))
 
 
 def rest_part(pos, q, kn, vn, o0, ml0, wo, k, v):
@@ -437,8 +447,8 @@
         ml, part, half = (2 * HEAD_PAD, 128), (span, 128), (n, d_model // 2)
         slab = half if kind == 'half' else (n, d_model // 4)
         shapes = dict(o=((2 * HEAD_PAD * n if own else 8, 128), F32), ml=(ml, F32),
-                      pml=(ml, F32), po=((2,) + part, F32), mlc=(ml, F32), oc=(part, F32), om=(part, F32),
-                      xo=(part, F32), xml=(ml, F32), ob=((n, rows_local), BF16), yq=(half, F32), yp=(half, F32),
+                      pml=(ml, F32), po=((2,) + part, F32), mlc=((16, 128), F32), mlo=((16, 128), F32), oc=(part, F32), om=(part, F32),
+                      xo=(part, F32), xml=((16, 128), F32), ob=((n, rows_local), BF16), yq=(half, F32), yp=(half, F32),
                       ym=(half, F32), yn=(slab if kind != 'half' else (8, 128), F32), yx=(slab, F32),
                       yxr=(slab, F32), yb=(slab, BF16), yg=(slab if kind == 'half' else (3,) + slab, BF16))
         return [pltpu.VMEM(*shapes[name]) for name in BUFS]
@@ -453,7 +463,7 @@
             pltpu.VMEM(wo.shape, BF16),
             pltpu.VMEM((BLOCK_ROWS, HEAD_PAD, seq_local), F32),
             pltpu.VMEM((BLOCK_ROWS, HEAD_PAD, seq_local), BF16),
-            pltpu.VMEM((5, HEAD_PAD, 128), F32),
+            pltpu.VMEM((4, HEAD_PAD, 128), F32),
             DMA, DMA((n_blocks,)), DMA((n_blocks,)), DMA((len(GROUPS), COPIES)), DMA((len(GROUPS), COPIES))]
             + [b for i, n in enumerate(GROUPS) for b in buffers(n, i > 0, KINDS[i])],
         compiler_params=pltpu.CompilerParams(collective_id=0, has_side_effects=True, vmem_limit_bytes=REST_VMEM * MIB),
@@ -470,32 +480,26 @@
     kret, vret = refs[2 * N_PIECES + 5:3 * N_PIECES + 5], refs[3 * N_PIECES + 5:4 * N_PIECES + 5]
     k_sems, v_sems, y_sem = refs[4 * N_PIECES + 5:]
     seq_local = ko_hbm.shape[1]
-    n_blocks = sum(PIECES) // BLOCK_ROWS
     base = lax.axis_index('sp') * seq_local
     write_y = pltpu.make_async_copy(y_ref, y_hbm, y_sem)
 
-    def writes(blk):
-        p = piece_of(blk)
-        src = pl.ds(blk * BLOCK_ROWS - PIECE_ROW0[p], BLOCK_ROWS)
-        dst = pl.ds(FIRST_ROWS + blk * BLOCK_ROWS, BLOCK_ROWS)
-        return (pltpu.make_async_copy(kret[p].at[src], ko_hbm.at[dst], k_sems.at[blk]),
-                pltpu.make_async_copy(vret[p].at[src], vo_hbm.at[dst], v_sems.at[blk]))
-
-    for blk in range(n_blocks):
-        p = piece_of(blk)
-        rows = pl.ds(blk * BLOCK_ROWS - PIECE_ROW0[p], BLOCK_ROWS)
-        for kept, new, copy in zip((kret, vret), (kn_ref, vn_ref), writes(blk)):
-            patch_rows(kept[p].at[rows], new, FIRST_ROWS + blk * BLOCK_ROWS, pos_ref, base, range(BLOCK_ROWS))
+    def writes(p):
+        dst = pl.ds(FIRST_ROWS + PIECE_ROW0[p], PIECES[p])
+        return (pltpu.make_async_copy(kret[p], ko_hbm.at[dst], k_sems.at[p]),
+                pltpu.make_async_copy(vret[p], vo_hbm.at[dst], v_sems.at[p]))
+
+    for p in range(N_PIECES):
+        for kept, new, copy in zip((kret, vret), (kn_ref, vn_ref), writes(p)):
+            patch_rows(kept[p], new, FIRST_ROWS + PIECE_ROW0[p], pos_ref, base, range(PIECES[p]))
             copy.start()
     write_y.start()
     write_y.wait()
-    for blk in range(n_blocks):
-        for c in writes(blk):
+    for p in range(N_PIECES):
+        for c in writes(p):
             c.wait()
 
 
 def write_part(pos, kn, vn, y, ko, vo, kret, vret):
-    n_blocks = sum(PIECES) // BLOCK_ROWS
     kept = (*kret, *vret)
     out = pl.pallas_call(
         write_kernel,
@@ -505,7 +509,7 @@
         out_specs=(ANY_SPEC, ANY_SPEC, ANY_SPEC) + (VMEM_SPEC,) * (2 * N_PIECES),
         input_output_aliases={4 + 2 * N_PIECES: 0, 5 + 2 * N_PIECES: 1,
                               **{4 + i: 3 + i for i in range(2 * N_PIECES)}},
-        scratch_shapes=[DMA((n_blocks,)), DMA((n_blocks,)), DMA],
+        scratch_shapes=[DMA((N_PIECES,)), DMA((N_PIECES,)), DMA],
         compiler_params=pltpu.CompilerParams(vmem_limit_bytes=REST_VMEM * MIB),
         cost_estimate=pl.CostEstimate(flops=10**10, bytes_accessed=40 * 10**6, transcendentals=0),
         name='attention_write',

time: 72.4 us -> 71.1 us (0.982)
  Pallas kernels: 71.7 us -> 70.2 us
    pallas_call x1, Pallas kernels: 31.6 us -> 30.6 us  [rest_part(): pl.pallas_call(rest_kernel, out_shape=tuple((pltpu.VMEM((n, seq_local, he...]
where the time goes in v3:
time: 71.1 us; the launch traced here: 71 us
  Pallas kernels  70.2 us (99%)
  between operations  0.82 us (1%)
    pallas_call x1, Pallas kernels, rest_part(): pl.pallas_call(rest_kernel, out_shape=tuple((pltpu.VMEM((n, seq_local, he...  30.6 us
    pallas_call x1, Pallas kernels, first_part(): pl.pallas_call(functools.partial(first_kernel, n_heads), out_shape=(jax.S...  27.6 us
    pallas_call x1, Pallas kernels, write_part(): pl.pallas_call(write_kernel, out_shape=(jax.ShapeDtypeStruct(ko.shape, ko...  11.9 us

profile of v3, /device:TPU:0, one launch (start us, length us, event | category | flops | bytes accessed | tf_op | source)
XLA Modules:
  0.0 71.0 jit_solution(14262579143484502737)
XLA Ops:
  0.6 0.0 copy-start
  0.6 27.6 %attention_first.1 = (bf16[128,512,256]{2,1,0:T(8,128)(2,1)}, bf16[128,512,256]{2,1,0:T(8,128)(2,1)}, f32[2,2048,128]{2,1,0:T(8,128)S(1)}, f32[128,256]{1,0:T(8,...) custom-call(s32[128]{0:T(128)} %pos_ref.5, bf16[128,2560]{1,0:T(8,128)(2,1)} %tok_hbm.1, ...), custom_call_target="tpu_custom_call" | custom-call | flops 10000000000 | bytes 70000000 | tf_op jit(solution)/shard_map/attention_first/pallas_call | solution.py:182
  28.3 0.0 copy-done
  28.3 30.6 %attention_rest.1 = (bf16[16,512,256]{2,1,0:T(8,128)(2,1)S(1)}, bf16[16,512,256]{2,1,0:T(8,128)(2,1)S(1)}, bf16[16,512,256]{2,1,0:T(8,128)(2,1)S(1)}, bf16[16,51...) custom-call(s32[128]{0:T(128)S(1)} %copy-done, ...), custom_call_target="tpu_custom_call" | custom-call | flops 10000000000 | bytes 40000000 | tf_op jit(solution)/shard_map/attention_rest/pallas_call | solution.py:456
  58.9 11.9 %attention_write.1 = (bf16[128,512,256]{2,1,0:T(8,128)(2,1)}, bf16[128,512,256]{2,1,0:T(8,128)(2,1)}, bf16[128,2560]{1,0:T(8,128)(2,1)}, bf16[16,512,256]{2,1,0:...) custom-call(s32[128]{0:T(128)S(1)} %copy-done, ...), custom_call_target="tpu_custom_call", output_to_operand_aliasing={{0}: (12, {}), {1}: (13, {}), {3}: (4, {}), {4}: (5, {}), {... | custom-call | flops 10000000000 | bytes 40000000 | tf_op jit(solution)/shard_map/attention_write/pallas_call | solution.py:504
Async XLA Ops:
  0.6 27.7 %copy-start = (s32[128]{0:T(128)S(1)}, s32[128]{0:T(128)}, u32[]{:S(2)}) copy-start(s32[128]{0:T(128)} %pos_ref.5) | copy-start | bytes 1540

commit v4 on v3

--- a/solution.py
+++ b/solution.py
@@ -11,8 +11,8 @@
 BF16 = jnp.bfloat16
 HEAD_PAD = 16
 BLOCK_ROWS = 8
-DMA_ROWS = 16
-EARLY = 2
+DMA_ROWS = 8
+EARLY = 5
 COL_CHUNK = 512
 PIECES = (16,) * 4
 FIRST_ROWS = 128 - sum(PIECES)

time: 71.1 us -> 70.9 us (level)
  no operation moved by 1% of the time
where the time goes in v4:
time: 70.9 us; the launch traced here: 70.8 us
  Pallas kernels  70.1 us (99%)
    pallas_call x1, Pallas kernels, rest_part(): pl.pallas_call(rest_kernel, out_shape=tuple((pltpu.VMEM((n, seq_local, he...  30.6 us
    pallas_call x1, Pallas kernels, first_part(): pl.pallas_call(functools.partial(first_kernel, n_heads), out_shape=(jax.S...  27.6 us
    pallas_call x1, Pallas kernels, write_part(): pl.pallas_call(write_kernel, out_shape=(jax.ShapeDtypeStruct(ko.shape, ko...  11.9 us

profile of v4, /device:TPU:0, one launch (start us, length us, event | category | flops | bytes accessed | tf_op | source)
XLA Modules:
  0.0 70.8 jit_solution(9390879657810026663)
XLA Ops:
  0.6 0.0 copy-start
  0.6 27.6 %attention_first.1 = (bf16[128,512,256]{2,1,0:T(8,128)(2,1)}, bf16[128,512,256]{2,1,0:T(8,128)(2,1)}, f32[2,2048,128]{2,1,0:T(8,128)S(1)}, f32[128,256]{1,0:T(8,...) custom-call(s32[128]{0:T(128)} %pos_ref.5, bf16[128,2560]{1,0:T(8,128)(2,1)} %tok_hbm.1, ...), custom_call_target="tpu_custom_call" | custom-call | flops 10000000000 | bytes 70000000 | tf_op jit(solution)/shard_map/attention_first/pallas_call | solution.py:182
  28.2 0.0 copy-done
  28.2 30.6 %attention_rest.1 = (bf16[16,512,256]{2,1,0:T(8,128)(2,1)S(1)}, bf16[16,512,256]{2,1,0:T(8,128)(2,1)S(1)}, bf16[16,512,256]{2,1,0:T(8,128)(2,1)S(1)}, bf16[16,51...) custom-call(s32[128]{0:T(128)S(1)} %copy-done, ...), custom_call_target="tpu_custom_call" | custom-call | flops 10000000000 | bytes 40000000 | tf_op jit(solution)/shard_map/attention_rest/pallas_call | solution.py:456
  58.9 11.9 %attention_write.1 = (bf16[128,512,256]{2,1,0:T(8,128)(2,1)}, bf16[128,512,256]{2,1,0:T(8,128)(2,1)}, bf16[128,2560]{1,0:T(8,128)(2,1)}, bf16[16,512,256]{2,1,0:...) custom-call(s32[128]{0:T(128)S(1)} %copy-done, ...), custom_call_target="tpu_custom_call", output_to_operand_aliasing={{0}: (12, {}), {1}: (13, {}), {3}: (4, {}), {4}: (5, {}), {... | custom-call | flops 10000000000 | bytes 40000000 | tf_op jit(solution)/shard_map/attention_write/pallas_call | solution.py:504
Async XLA Ops:
  0.6 27.6 %copy-start = (s32[128]{0:T(128)S(1)}, s32[128]{0:T(128)}, u32[]{:S(2)}) copy-start(s32[128]{0:T(128)} %pos_ref.5) | copy-start | bytes 1540
